TPU v7x, 32 devices: a whole 2x2x4 slice. The times are simulated.
32 devices in a mesh: groups: 2 (over x), feat: 16 (over z, y, core).
Axes of the slice: x: 2, y: 2, z: 4, core: 2. Of those that a mesh axis runs over, the one named last changes fastest.
Arguments:
- cells: bfloat16 [96, 512, 192], P('groups', 'feat'), parts along dimension 0, may hold values from -6 to 6
- missing: int32 [96, 512], P('groups', 'feat'), parts along dimension 0, may hold values 0 or 1
- feat_ids: int32 [1024], P(('groups', 'feat')), parts along dimension 0, may hold values from 0 to 63
- feat_table: float32 [64, 192], replicated, may hold values from -5 to 5
- nan_embed: float32 [192], replicated, may hold values from -5 to 5
- gain_one: float32 [192], replicated, may hold values from 0.1 to 1.9
- w_qkv: bfloat16 [192, 576], replicated, may hold values from -3 to 3
- w_out: bfloat16 [192, 192], replicated, may hold values from -0.4375 to 0.4375
- gain_two: float32 [192], replicated, may hold values from 0.1 to 1.9
- w_up: bfloat16 [192, 768], replicated, may hold values from -0.4375 to 0.4375
- w_down: bfloat16 [768, 192], replicated, may hold values from -0.21875 to 0.21875
Outputs:
- result: float32 [96, 512, 192], P('groups', 'feat'), parts along dimension 0
There are 2 independent parts, one for each index of `groups`. A program takes and returns all parts, laid end to end along the dimension named above; an argument that names none is the same for every part. Nothing has to cross between parts.
All inputs are finite; a program needn't handle non-finite values. No bound on the sum of `missing` on one device may be relied on, other than what follows from the above.
Results may differ from a plain program's by a relative error of at most 0.007.
The roundings to bfloat16 on the way count: a program that leaves them out, or rounds other values in their place, can miss the bound.
Values may be sent and summed in bfloat16 or wider, within the bound.
A program may use at most 64 MiB of HBM per device.

v0:
```python
import functools
import math

import jax
import jax.numpy as jnp
from jax import lax
from jax.experimental import pallas as pl
from jax.experimental.pallas import tpu as pltpu
from jax.sharding import PartitionSpec as P

HEADS = 6
MESH = pl.DeviceIdType.MESH
F32 = jnp.float32
BF16 = jnp.bfloat16
LIMIT = 60 * 1024 * 1024


def cell_norm(values, gain):
    mean = jnp.mean(values, axis=-1, keepdims=True)
    centered = values - mean
    var = jnp.mean(centered * centered, axis=-1, keepdims=True)
    return (centered * lax.rsqrt(var + 1e-05) * gain).astype(BF16)


def pack(values, packed):
    if not packed:
        return values
    half = values.shape[-2] // 2
    tail = values[..., 128:]
    tail = jnp.concatenate([tail[..., :half, :], tail[..., half:, :]], axis=-1)
    return jnp.concatenate([values[..., :128], tail], axis=-2)


def unpack(values, feats, width, packed):
    if packed:
        rest = width - 128
        tail = values[:, feats:]
        tail = jnp.concatenate([tail[..., :rest], tail[..., rest:]], axis=-2)
        values = jnp.concatenate([values[:, :feats], tail], axis=-1)
    return values.reshape(values.shape[0] * feats, width)


def attend(normed, wk, wqv_t):
    width = wk.shape[0]
    head_dim = width // HEADS
    count = normed.shape[0]
    keys = jnp.dot(normed, wk, preferred_element_type=F32).astype(BF16)
    turned = lax.dot_general(
        wqv_t, normed, (((1,), (1,)), ((), ())), preferred_element_type=F32
    ).astype(BF16)
    scale = head_dim ** (-0.5) * math.log2(math.e)
    ones = jnp.ones((16, count), BF16)
    outs = []
    for head in range(HEADS):
        low = head * head_dim
        block = low // 128 * 128
        high = min(block + 128, width)
        parts = []
        if low > block:
            parts.append(jnp.zeros((low - block, count), BF16))
        parts.append(turned[low : low + head_dim])
        if high > low + head_dim:
            parts.append(jnp.zeros((high - low - head_dim, count), BF16))
        query = jnp.concatenate(parts, axis=0)
        scores = jnp.dot(keys[:, block:high], query, preferred_element_type=F32)
        top = jnp.max(scores, axis=0, keepdims=True)
        expo = jnp.exp2((scores - top) * scale).astype(BF16)
        values = jnp.concatenate([turned[width + low : width + low + head_dim], ones], axis=0)
        sums = jnp.dot(values, expo, preferred_element_type=F32)
        outs.append(sums[:head_dim] / sums[head_dim : head_dim + 1])
    return jnp.concatenate(outs, axis=0).T


def kernel(n, rows, feats, width, packed, *refs):
    sources, refs = refs[:11], refs[11:]
    out, held, refs = refs[0], refs[1:12], refs[12:]
    tok, got, ctx, back, wqv_t, done, load_sems, send_sems, recv_sems, out_sems = refs
    (cells, missing, feat_ids, feat_table, nan_embed) = held[:5]
    (gain_one, w_qkv, w_out, gain_two, w_up, w_down) = held[5:]
    me = lax.axis_index("feat")
    barrier = pltpu.get_barrier_semaphore()

    def greet(step, carry):
        peer = lax.rem(me + step, n)
        pl.semaphore_signal(barrier, inc=1, device_id={"feat": peer}, device_id_type=MESH)
        return carry

    lax.fori_loop(1, n, greet, 0)

    loads = [
        pltpu.make_async_copy(source, target, load_sems.at[spot])
        for spot, (source, target) in enumerate(zip(sources, held))
    ]
    for load in loads:
        load.start()
    for load in loads[:5]:
        load.wait()

    ncat = feat_table.shape[0]
    hot = (lax.broadcasted_iota(jnp.int32, (ncat, feats), 0) == feat_ids[...]).astype(F32)
    femb = lax.dot_general(
        hot, feat_table[...], (((0,), (0,)), ((), ())),
        precision=lax.Precision.HIGHEST, preferred_element_type=F32,
    )
    nan = nan_embed[...]
    absent = missing[...].astype(F32)
    def spread(source, target, kind, row):
        def one(step, carry):
            peer = lax.rem(me + step, n)
            pltpu.make_async_remote_copy(
                src_ref=source.at[row, peer],
                dst_ref=target.at[row, me],
                send_sem=send_sems.at[kind, row],
                recv_sem=recv_sems.at[kind, row],
                device_id={"feat": peer},
                device_id_type=MESH,
            ).start()
            return carry

        lax.fori_loop(1, n, one, 0)

    def settle(ref, sems, kind, row):
        piece = ref.at[row, pl.ds(0, n - 1)]
        pltpu.make_async_copy(piece, piece, sems.at[kind, row]).wait()

    for row in range(rows):
        for peer in range(n):
            spot = peer * rows + row
            values = cells[peer, row].astype(F32)
            values = (values + absent[:, spot : spot + 1] * nan + femb).astype(BF16)
            tok[row, peer] = pack(values, packed)
        if row == 0:
            pl.semaphore_wait(barrier, n - 1)
        spread(tok, got, 0, row)
    for row in range(rows):
        got[row, pl.ds(me, 1)] = tok[row, pl.ds(me, 1)]
    for load in loads[5:]:
        load.wait()
    wqv_t[0:width] = w_qkv[:, :width].astype(F32).T.astype(BF16)
    wqv_t[width:] = w_qkv[:, 2 * width :].astype(F32).T.astype(BF16)

    def attention(row, carry):
        settle(got, recv_sems, 0, row)
        base = unpack(got[row].astype(F32), feats, width, packed)
        normed = cell_norm(base, gain_one[...])
        context = attend(normed, w_qkv[:, width : 2 * width], wqv_t[...])
        sent = pack(context.reshape(n, feats, width), packed).astype(BF16)
        ctx[row] = sent
        spread(ctx, back, 1, row)
        back[row, pl.ds(me, 1)] = ctx[row, pl.ds(me, 1)]
        return carry

    lax.fori_loop(0, rows, attention, 0)

    def store(row):
        return pltpu.make_async_copy(done.at[row], out.at[:, row], out_sems.at[row])

    def finish(row, carry):
        settle(back, recv_sems, 1, row)
        context = unpack(back[row].astype(F32), feats, width, packed).astype(BF16)
        base = unpack(tok[row].astype(F32), feats, width, packed)
        mid = base + jnp.dot(context, w_out[...], preferred_element_type=F32)
        normed = cell_norm(mid, gain_two[...])
        hidden = jnp.dot(normed, w_up[...], preferred_element_type=F32)
        act = (0.5 * hidden * (1.0 + lax.erf(hidden * math.sqrt(0.5)))).astype(BF16)
        result = mid + lax.dot_general(
            act, w_down[...], (((1,), (1,)), ((), ())), preferred_element_type=F32
        )
        done[row] = result.reshape(n, feats, width)
        store(row).start()
        return carry

    lax.fori_loop(0, rows, finish, 0)

    for row in range(rows):
        settle(tok, send_sems, 0, row)
        settle(ctx, send_sems, 1, row)
        store(row).wait()


def body(
    cells, missing, feat_ids, feat_table, nan_embed, gain_one, w_qkv, w_out, gain_two, w_up, w_down
):
    n = lax.axis_size("feat")
    all_rows, feats, width = cells.shape
    rows = all_rows // n
    packed = width == 192 and feats % 32 == 0
    piece = (feats + feats // 2, 128) if packed else (feats, width)
    buffer = pltpu.VMEM((rows, n) + piece, BF16)
    operands = (
        cells.reshape(n, rows, feats, width),
        missing.T,
        feat_ids[None],
        feat_table,
        nan_embed[None],
        gain_one[None],
        w_qkv,
        w_out,
        gain_two[None],
        w_up,
        w_down.T,
    )
    result = pl.pallas_call(
        functools.partial(kernel, n, rows, feats, width, packed),
        out_shape=jax.ShapeDtypeStruct((n, rows, feats, width), F32),
        in_specs=[pl.BlockSpec(memory_space=pltpu.HBM)] * len(operands),
        out_specs=pl.BlockSpec(memory_space=pltpu.HBM),
        scratch_shapes=[pltpu.VMEM(x.shape, x.dtype) for x in operands]
        + [
            buffer,
            buffer,
            buffer,
            buffer,
            pltpu.VMEM((2 * width, width), BF16),
            pltpu.VMEM((rows, n, feats, width), F32),
            pltpu.SemaphoreType.DMA((len(operands),)),
            pltpu.SemaphoreType.DMA((2, rows)),
            pltpu.SemaphoreType.DMA((2, rows)),
            pltpu.SemaphoreType.DMA((rows,)),
        ],
        compiler_params=pltpu.CompilerParams(
            collective_id=0, has_side_effects=True, vmem_limit_bytes=LIMIT
        ),
    )(*operands)
    return result.reshape(all_rows, feats, width)


def solution(mesh):
    in_specs = (
        P("groups", "feat", None),
        P("groups", "feat"),
        P(("groups", "feat")),
        P(),
        P(),
        P(),
        P(),
        P(),
        P(),
        P(),
        P(),
    )
    out_specs = P("groups", "feat", None)
    return jax.shard_map(body, mesh=mesh, in_specs=in_specs, out_specs=out_specs, check_vma=False)
```

profile of v0, /device:TPU:0, one launch (start us, length us, event | category | flops | bytes accessed | tf_op | source)
XLA Modules:
  0.0 36.2 jit_solution(15683318160216526523)
XLA Ops:
  0.0 33.5 %shard_map.109 = f32[16,3,32,192]{3,2,1,0:T(8,128)} custom-call(bf16[16,3,32,192]{3,2,1,0:T(8,128)(2,1)} %bitcast.9, s32[32,48]{1,0:T(8,128)} %bitcast.11, s32[1,32]{1,0:T(1,128)} %bitcast.15, f32[64,192]{1,0:T(8,128)} %refs_3_.1, f32[1,192]{1,0:T(1,128)} %bitcast.12, f32[1,192]{1,0:T(1,128)} %bitcast.13, bf16[192,576]{1,0:T(8,128)(2,1)} %refs_6_.1, ...), custom_call_target="tpu_custom_call" | custom-call | tf_op jit(solution)/shard_map/pallas_call | solution.py:203
  33.5 2.7 %copy.13 = f32[48,32,192]{2,1,0:T(8,128)} copy(f32[48,32,192]{2,1,0:T(8,128)} %bitcast.8) | data formatting | bytes 2359296
where the time goes:
time: 36.4 us; the launch traced here: 36.2 us
  Pallas kernels  33.5 us (92%)
  local copies, waits for them, and re-layouts  2.73 us (8%)
    pallas_call x1, Pallas kernels, body(): pl.pallas_call(functools.partial(kernel, n, rows, feats, width, packed),...  33.5 us
    unnamed x1, local copies, waits for them, and re-layouts  2.73 us

commit v1 on v0

--- a/solution.py
+++ b/solution.py
@@ -202,9 +202,9 @@
     )
     result = pl.pallas_call(
         functools.partial(kernel, n, rows, feats, width, packed),
-        out_shape=jax.ShapeDtypeStruct((n, rows, feats, width), F32),
+        out_shape=pltpu.VMEM((n, rows, feats, width), F32),
         in_specs=[pl.BlockSpec(memory_space=pltpu.HBM)] * len(operands),
-        out_specs=pl.BlockSpec(memory_space=pltpu.HBM),
+        out_specs=pl.BlockSpec(memory_space=pltpu.VMEM),
         scratch_shapes=[pltpu.VMEM(x.shape, x.dtype) for x in operands]
         + [
             buffer,

time: 36.4 us -> 34 us (0.934)
  local copies, waits for them, and re-layouts: 2.73 us -> 1.15 us
  Pallas kernels: 33.5 us -> 32.8 us
    unnamed x1, local copies, waits for them, and re-layouts: 2.73 us -> 1.15 us
    pallas_call x1, Pallas kernels: 33.5 us -> 32.8 us  [body(): pl.pallas_call(functools.partial(kernel, n, rows, feats, width, packed),...]
where the time goes in v1:
time: 34 us; the launch traced here: 33.9 us
  Pallas kernels  32.8 us (96%)
  local copies, waits for them, and re-layouts  1.15 us (3%)
    pallas_call x1, Pallas kernels, body(): pl.pallas_call(functools.partial(kernel, n, rows, feats, width, packed),...  32.8 us
    unnamed x1, local copies, waits for them, and re-layouts  1.15 us

profile of v1, /device:TPU:0, one launch (start us, length us, event | category | flops | bytes accessed | tf_op | source)
XLA Modules:
  0.0 33.9 jit_solution(11824770810420002650)
XLA Ops:
  0.0 32.8 %shard_map.109 = f32[16,3,32,192]{3,2,1,0:T(8,128)S(1)} custom-call(bf16[16,3,32,192]{3,2,1,0:T(8,128)(2,1)} %bitcast.9, s32[32,48]{1,0:T(8,128)} %bitcast.11, s32[1,32]{1,0:T(1,128)} %bitcast.15, f32[64,192]{1,0:T(8,128)} %refs_3_.1, f32[1,192]{1,0:T(1,128)} %bitcast.12, f32[1,192]{1,0:T(1,128)} %bitcast.13, bf16[192,576]{1,0:T(8,128)(2,1)} %refs_6_.1, ...), custom_call_target="tpu_custom_call" | custom-call | tf_op jit(solution)/shard_map/pallas_call | solution.py:203
  32.8 1.1 %copy.13 = f32[48,32,192]{2,1,0:T(8,128)} copy(f32[48,32,192]{2,1,0:T(8,128)S(1)} %bitcast.8) | data formatting | bytes 2359296

commit v2 on v1

v2 whole, which is shorter than its diff:
```python
import functools
import math

import jax
import jax.numpy as jnp
from jax import lax
from jax.experimental import pallas as pl
from jax.experimental.pallas import tpu as pltpu
from jax.sharding import PartitionSpec as P

HEADS = 6
MESH = pl.DeviceIdType.MESH
F32 = jnp.float32
BF16 = jnp.bfloat16
LIMIT = 58 * 1024 * 1024


def cell_norm(values, gain):
    mean = jnp.mean(values, axis=-1, keepdims=True)
    centered = values - mean
    var = jnp.mean(centered * centered, axis=-1, keepdims=True)
    return (centered * lax.rsqrt(var + 1e-05) * gain).astype(BF16)


def pack(values, packed):
    if not packed:
        return values
    half = values.shape[-2] // 2
    tail = values[..., 128:]
    tail = jnp.concatenate([tail[..., :half, :], tail[..., half:, :]], axis=-1)
    return jnp.concatenate([values[..., :128], tail], axis=-2)


def unpack(values, feats, width, packed):
    if packed:
        rest = width - 128
        tail = values[:, feats:]
        tail = jnp.concatenate([tail[..., :rest], tail[..., rest:]], axis=-2)
        values = jnp.concatenate([values[:, :feats], tail], axis=-1)
    return values.reshape(values.shape[0] * feats, width)


def lanes(head, head_dim, width):
    low = head * head_dim
    block = low // 128 * 128
    return low, block, min(block + 128, width)


def project(normed, wk, wqv_t, keys, query, value, first, count):
    width = wk.shape[0]
    head_dim = width // HEADS
    here = slice(first, first + count)
    keys[here] = jnp.dot(normed, wk, preferred_element_type=F32).astype(BF16)
    turned = lax.dot_general(
        wqv_t, normed, (((1,), (1,)), ((), ())), preferred_element_type=F32
    ).astype(BF16)
    for head in range(HEADS):
        low, block, high = lanes(head, head_dim, width)
        query[head, low - block : low - block + head_dim, here] = turned[low : low + head_dim]
        value[head, 0:head_dim, here] = turned[width + low : width + low + head_dim]


def score(keys, query, head, width):
    _, block, high = lanes(head, width // HEADS, width)
    return jnp.dot(
        keys[:, block:high], query[head, 0 : high - block], preferred_element_type=F32
    )


def weigh(scores, value, head, head_dim):
    scale = head_dim ** (-0.5) * math.log2(math.e)
    top = jnp.max(scores, axis=0, keepdims=True)
    expo = jnp.exp2((scores - top) * scale).astype(BF16)
    sums = jnp.dot(value[head], expo, preferred_element_type=F32)
    return sums[:head_dim] / sums[head_dim : head_dim + 1]


def feed(context, base, w_out, gain_two, w_up, w_down, feats, width, packed):
    context = unpack(context.astype(F32), feats, width, packed).astype(BF16)
    base = unpack(base.astype(F32), feats, width, packed)
    mid = base + jnp.dot(context, w_out[...], preferred_element_type=F32)
    normed = cell_norm(mid, gain_two[...])
    hidden = jnp.dot(normed, w_up[...], preferred_element_type=F32)
    act = (0.5 * hidden * (1.0 + lax.erf(hidden * math.sqrt(0.5)))).astype(BF16)
    return mid + lax.dot_general(
        act, w_down[...], (((1,), (1,)), ((), ())), preferred_element_type=F32
    )


def close(n, rows, feats, width, packed, *refs):
    done, back, tok, w_out, gain_two, w_up, w_down, out, last, sems = refs
    half = n // 2
    mine = lax.axis_index("feat") // half * half
    other = half - mine
    final = rows - 1
    copies = [
        pltpu.make_async_copy(done.at[row], out.at[:, row], sems.at[row]) for row in range(final)
    ]
    here = pl.ds(mine, half)
    copies.append(pltpu.make_async_copy(done.at[final, here], out.at[here, final], sems.at[final]))
    for copy in copies:
        copy.start()
    here = pl.ds(other, half)
    last[...] = feed(
        back[final, here], tok[final, here], w_out, gain_two, w_up, w_down, feats, width, packed
    ).reshape(half, feats, width)
    copies.append(pltpu.make_async_copy(last, out.at[here, final], sems.at[rows]))
    copies[-1].start()
    for copy in copies:
        copy.wait()


def kernel(n, rows, feats, width, packed, *refs):
    sources, refs = refs[:11], refs[11:]
    done, back, tok, w_out, gain_two, w_up, w_down = refs[:7]
    held, refs = refs[7:14] + (w_out, gain_two, w_up, w_down), refs[14:]
    got, ctx, wqv_t, keys, query, value, turned, even, odd, load_sems, cell_sems, send_sems, recv_sems, all_sem = refs
    (cells, missing, feat_ids, feat_table, nan_embed) = held[:5]
    gain_one, w_qkv = held[5:7]
    scores = (even, odd)
    me = lax.axis_index("feat")
    half = n // 2
    quarter = half // 2
    mine = me // half * half
    other = half - mine
    high = me >= half
    barrier = pltpu.get_barrier_semaphore()

    def greet(peer):
        pl.semaphore_signal(barrier, inc=1, device_id={"feat": peer}, device_id_type=MESH)

    def greet_other(step, carry):
        greet(other + step)
        return carry

    def greet_mine(step, carry):
        greet(mine + lax.rem(me - mine + step, half))
        return carry

    def greet_near():
        lax.fori_loop(1, half, greet_mine, 0)

    lax.fori_loop(0, half, greet_other, 0)
    pl.when(jnp.logical_not(high))(greet_near)

    cell_loads = [
        pltpu.make_async_copy(sources[0].at[:, row], cells.at[:, row], cell_sems.at[row])
        for row in range(rows)
    ]
    loads = [
        pltpu.make_async_copy(source, target, load_sems.at[spot])
        for spot, (source, target) in enumerate(zip(sources[1:], held[1:]))
    ]
    for load in loads[:4] + cell_loads[:1] + loads[4:5] + cell_loads[1:] + loads[5:]:
        load.start()
    for load in loads[:4]:
        load.wait()

    ncat = feat_table.shape[0]
    hot = (lax.broadcasted_iota(jnp.int32, (ncat, feats), 0) == feat_ids[...]).astype(F32)
    femb = lax.dot_general(
        hot, feat_table[...], (((0,), (0,)), ((), ())),
        precision=lax.Precision.HIGHEST, preferred_element_type=F32,
    )
    nan = nan_embed[...]
    absent = missing[...].astype(F32)

    def give(source, target, kind, row, side, peer):
        pltpu.make_async_remote_copy(
            src_ref=source.at[row, peer],
            dst_ref=target.at[row, me],
            send_sem=send_sems.at[kind, row],
            recv_sem=recv_sems.at[kind, row, side],
            device_id={"feat": peer},
            device_id_type=MESH,
        ).start()

    def spread(source, target, kind, row):
        def one(step, carry):
            peer = me + step
            peer = jnp.where(peer < n, peer, peer - n)
            side = jnp.where((peer >= mine) & (peer < mine + half), 0, 1)
            give(source, target, kind, row, side, peer)
            return carry

        lax.fori_loop(1, n, one, 0)

    def settle(ref, sem, row, count):
        piece = ref.at[row, pl.ds(0, count)]
        pltpu.make_async_copy(piece, piece, sem).wait()

    def arrive(ref, kind, row, side):
        settle(ref, recv_sems.at[kind, row, side], row, half - 1 + side)

    def build(row, peer):
        spot = peer * rows + row
        values = cells[peer, row].astype(F32)
        values = (values + absent[:, spot : spot + 1] * nan + femb).astype(BF16)
        tok[row, peer] = pack(values, packed)

    def open_high():
        pl.semaphore_wait(barrier, half)

    cell_loads[0].wait()
    pl.when(high)(open_high)
    for peer in range(n):
        build(0, peer)
        if peer < half:
            pl.when(high)(lambda peer=peer: give(tok, got, 0, 0, 1, peer))
    for row in range(1, rows):
        cell_loads[row].wait()
        for peer in range(n):
            build(row, peer)

    def near(step, carry):
        give(tok, got, 0, 0, 0, mine + lax.rem(me - mine + step, half))
        return carry

    def open_low():
        pl.semaphore_wait(barrier, n - 1)

    def tell(ahead):
        pl.semaphore_signal(
            all_sem, inc=1, device_id={"feat": me + ahead}, device_id_type=MESH
        )

    def tell_high():
        tell(quarter)
        tell(half)

    def first_low():
        spread(tok, got, 0, 0)

    def first_high():
        pl.semaphore_wait(all_sem, 1)
        lax.fori_loop(1, half, near, 0)

    low = jnp.logical_not(high)
    pl.when(low)(open_low)
    pl.when(low & (me >= half - quarter))(tell_high)
    pl.when(low)(first_low)
    pl.when(high)(first_high)
    for row in range(1, rows):
        spread(tok, got, 0, row)
    for row in range(rows):
        got[row, pl.ds(me, 1)] = tok[row, pl.ds(me, 1)]
    for load in loads[4:]:
        load.wait()
    gain = gain_one[...]
    wqv_t[0:width] = w_qkv[:, :width].astype(F32).T.astype(BF16)
    wqv_t[width:] = w_qkv[:, 2 * width :].astype(F32).T.astype(BF16)

    head_dim = width // HEADS
    count = n * feats
    query[...] = jnp.zeros_like(query)
    value[...] = jnp.ones_like(value)

    def attention(row, carry):
        arrive(got, 0, row, 0)
        arrive(got, 0, row, 1)
        normed = cell_norm(unpack(got[row].astype(F32), feats, width, packed), gain)
        project(normed, w_qkv[:, width : 2 * width], wqv_t[...], keys, query, value, 0, count)
        scores[0][...] = score(keys, query, 0, width)
        for head in range(HEADS):
            if head + 1 < HEADS:
                scores[(head + 1) % 2][...] = score(keys, query, head + 1, width)
            turned[head * head_dim : (head + 1) * head_dim] = weigh(
                scores[head % 2][...], value, head, head_dim
            )
        context = turned[...].T
        ctx[row] = pack(context.reshape(n, feats, width), packed).astype(BF16)
        spread(ctx, back, 1, row)
        back[row, pl.ds(me, 1)] = ctx[row, pl.ds(me, 1)]
        return carry

    lax.fori_loop(0, rows, attention, 0)

    def finish(row, first, count):
        here = pl.ds(first, count)
        done[row, here] = feed(
            back[row, here], tok[row, here], w_out, gain_two, w_up, w_down, feats, width, packed
        ).reshape(count, feats, width)

    def whole(row, carry):
        arrive(back, 1, row, 0)
        arrive(back, 1, row, 1)
        finish(row, 0, n)
        return carry

    lax.fori_loop(0, rows - 1, whole, 0)
    arrive(back, 1, rows - 1, 0)
    finish(rows - 1, mine, half)
    arrive(back, 1, rows - 1, 1)
    for row in range(rows):
        settle(tok, send_sems.at[0, row], row, n - 1)
        settle(ctx, send_sems.at[1, row], row, n - 1)


def body(
    cells, missing, feat_ids, feat_table, nan_embed, gain_one, w_qkv, w_out, gain_two, w_up, w_down
):
    n = lax.axis_size("feat")
    all_rows, feats, width = cells.shape
    rows = all_rows // n
    packed = width == 192 and feats % 32 == 0
    piece = (feats + feats // 2, 128) if packed else (feats, width)
    buffer = pltpu.VMEM((rows, n) + piece, BF16)
    operands = (
        cells.reshape(n, rows, feats, width),
        missing.T,
        feat_ids[None],
        feat_table,
        nan_embed[None],
        gain_one[None],
        w_qkv,
        w_out,
        gain_two[None],
        w_up,
        w_down.T,
    )
    kept = pltpu.VMEM((rows, n) + piece, BF16)
    results = pl.pallas_call(
        functools.partial(kernel, n, rows, feats, width, packed),
        out_shape=[pltpu.VMEM((rows, n, feats, width), F32), kept, kept]
        + [pltpu.VMEM(x.shape, x.dtype) for x in operands[7:]],
        in_specs=[pl.BlockSpec(memory_space=pltpu.HBM)] * len(operands),
        out_specs=[pl.BlockSpec(memory_space=pltpu.VMEM)] * 7,
        scratch_shapes=[pltpu.VMEM(x.shape, x.dtype) for x in operands[:7]]
        + [
            buffer,
            buffer,
            pltpu.VMEM((2 * width, width), BF16),
            pltpu.VMEM((n * feats, width), BF16),
            pltpu.VMEM((HEADS, 128, n * feats), BF16),
            pltpu.VMEM((HEADS, width // HEADS + 16, n * feats), BF16),
            pltpu.VMEM((width, n * feats), F32),
            pltpu.VMEM((n * feats, n * feats), F32),
            pltpu.VMEM((n * feats, n * feats), F32),
            pltpu.SemaphoreType.DMA((len(operands) - 1,)),
            pltpu.SemaphoreType.DMA((rows,)),
            pltpu.SemaphoreType.DMA((2, rows)),
            pltpu.SemaphoreType.DMA((2, rows, 2)),
            pltpu.SemaphoreType.REGULAR,
        ],
        compiler_params=pltpu.CompilerParams(
            collective_id=0, has_side_effects=True, vmem_limit_bytes=LIMIT
        ),
    )(*operands)
    result = pl.pallas_call(
        functools.partial(close, n, rows, feats, width, packed),
        out_shape=jax.ShapeDtypeStruct((n, rows, feats, width), F32),
        in_specs=[pl.BlockSpec(memory_space=pltpu.VMEM)] * 7,
        out_specs=pl.BlockSpec(memory_space=pltpu.HBM),
        scratch_shapes=[
            pltpu.VMEM((n // 2, feats, width), F32),
            pltpu.SemaphoreType.DMA((rows + 1,)),
        ],
        compiler_params=pltpu.CompilerParams(vmem_limit_bytes=8 * 1024 * 1024),
    )(*results)
    return result.reshape(all_rows, feats, width)


def solution(mesh):
    in_specs = (
        P("groups", "feat", None),
        P("groups", "feat"),
        P(("groups", "feat")),
        P(),
        P(),
        P(),
        P(),
        P(),
        P(),
        P(),
        P(),
    )
    out_specs = P("groups", "feat", None)
    return jax.shard_map(body, mesh=mesh, in_specs=in_specs, out_specs=out_specs, check_vma=False)
```

time: 34 us -> 32.8 us (0.965)
  local copies, waits for them, and re-layouts: 1.15 us -> 0 us
    pallas_call x1, Pallas kernels: 32.8 us -> 31 us  [body(): pl.pallas_call(functools.partial(kernel, n, rows, feats, width, packed),...]
    pallas_call x0 -> x1, Pallas kernels: none -> 1.59 us  [body(): pl.pallas_call(functools.partial(close, n, rows, feats, width, packed), o...]
    unnamed x1 -> x0, local copies, waits for them, and re-layouts: 1.15 us -> none
where the time goes in v2:
time: 32.8 us; the launch traced here: 32.6 us
  Pallas kernels  32.6 us (99%)
    pallas_call x1, Pallas kernels, body(): pl.pallas_call(functools.partial(kernel, n, rows, feats, width, packed),...  31 us
    pallas_call x1, Pallas kernels, body(): pl.pallas_call(functools.partial(close, n, rows, feats, width, packed), o...  1.59 us

profile of v2, /device:TPU:0, one launch (start us, length us, event | category | flops | bytes accessed | tf_op | source)
XLA Modules:
  0.0 32.6 jit_solution(12359530737698395738)
XLA Ops:
  0.0 31.0 %shard_map.109 = (f32[3,16,32,192]{3,2,1,0:T(8,128)S(1)}, bf16[3,16,48,128]{3,2,1,0:T(8,128)(2,1)S(1)}, bf16[3,16,48,128]{3,2,1,0:T(8,128)(2,1)S(1)}, bf16[192,1...) custom-call(bf16[16,3,32,192]{3,2,1,0:T(8,128)(2,1)} %bitcast.8, ...), custom_call_target="tpu_custom_call" | custom-call | tf_op jit(solution)/shard_map/pallas_call | solution.py:322
  31.0 1.6 %shard_map.110 = f32[16,3,32,192]{3,2,1,0:T(8,128)} custom-call(f32[3,16,32,192]{3,2,1,0:T(8,128)S(1)} %get-tuple-element.12.refs_0_, bf16[3,16,48,128]{3,2,1,0:T(8,128)(2,1)S(1)} %get-tuple-element.13.refs_1_, bf16[3,16,48,128]{3,2,1,0:T(8,128)(2,1)S(1)} %get-tuple-element.14.refs_2_, bf16[192,192]{1,0:T(8,128)(2,1)S(1)} %get-tuple-element.15.refs_3_, ...), custom_call_target="tpu_custom_call" | custom-call | tf_op jit(solution)/shard_map/pallas_call | solution.py:349

commit v3 on v2

--- a/solution.py
+++ b/solution.py
@@ -90,17 +90,20 @@
 def close(n, rows, feats, width, packed, *refs):
     done, back, tok, w_out, gain_two, w_up, w_down, out, last, sems = refs
     half = n // 2
-    mine = lax.axis_index("feat") // half * half
+    quarter = half // 2
+    me = lax.axis_index("feat")
+    mine = me // half * half
     other = half - mine
+    inner_high = me // quarter == 2
     final = rows - 1
     copies = [
         pltpu.make_async_copy(done.at[row], out.at[:, row], sems.at[row]) for row in range(final)
     ]
-    here = pl.ds(mine, half)
+    here = pl.ds(jnp.where(inner_high, other, mine), half)
     copies.append(pltpu.make_async_copy(done.at[final, here], out.at[here, final], sems.at[final]))
     for copy in copies:
         copy.start()
-    here = pl.ds(other, half)
+    here = pl.ds(jnp.where(inner_high, mine, other), half)
     last[...] = feed(
         back[final, here], tok[final, here], w_out, gain_two, w_up, w_down, feats, width, packed
     ).reshape(half, feats, width)
@@ -126,22 +129,23 @@
     high = me >= half
     barrier = pltpu.get_barrier_semaphore()
 
-    def greet(peer):
-        pl.semaphore_signal(barrier, inc=1, device_id={"feat": peer}, device_id_type=MESH)
-
-    def greet_other(step, carry):
-        greet(other + step)
-        return carry
-
-    def greet_mine(step, carry):
-        greet(mine + lax.rem(me - mine + step, half))
-        return carry
-
-    def greet_near():
-        lax.fori_loop(1, half, greet_mine, 0)
-
-    lax.fori_loop(0, half, greet_other, 0)
-    pl.when(jnp.logical_not(high))(greet_near)
+    part = me // quarter
+    inner_low = part == 1
+    inner_high = part == 2
+    outer = (part == 0) | (part == 3)
+
+    def greet(first, skip):
+        def one(step, carry):
+            peer = first + lax.rem(me - part * quarter + step, quarter)
+            pl.semaphore_signal(barrier, inc=1, device_id={"feat": peer}, device_id_type=MESH)
+            return carry
+
+        lax.fori_loop(skip, quarter, one, 0)
+
+    pl.when(me < half)(lambda: greet(half, 0))
+    pl.when(inner_high)(lambda: greet(quarter, 0))
+    greet(0, jnp.where(part == 0, 1, 0))
+    greet(half + quarter, jnp.where(part == 3, 1, 0))
 
     cell_loads = [
         pltpu.make_async_copy(sources[0].at[:, row], cells.at[:, row], cell_sems.at[row])
@@ -198,48 +202,71 @@
         values = (values + absent[:, spot : spot + 1] * nan + femb).astype(BF16)
         tok[row, peer] = pack(values, packed)
 
+    def tell(ahead):
+        pl.semaphore_signal(
+            all_sem, inc=1, device_id={"feat": me - ahead}, device_id_type=MESH
+        )
+
+    def open_outer():
+        pl.semaphore_wait(barrier, n - 1)
+
+    def tell_inner():
+        tell(quarter)
+        tell(half)
+
     def open_high():
         pl.semaphore_wait(barrier, half)
 
+    def open_low():
+        pl.semaphore_wait(barrier, quarter)
+        lax.fori_loop(0, quarter, across, 0)
+
+    def across(step, carry):
+        give(tok, got, 0, 0, 1, half + lax.rem(me + step, quarter))
+        return carry
+
+    def beyond(step, carry):
+        give(tok, got, 0, 0, 1, half + quarter + lax.rem(me + step, quarter))
+        return carry
+
+    def near(step, carry):
+        give(tok, got, 0, 0, 0, mine + lax.rem(me - mine + step, half))
+        return carry
+
+    def wait_all():
+        pl.semaphore_wait(all_sem, 1)
+
+    def open_last():
+        open_outer()
+        tell_inner()
+
     cell_loads[0].wait()
-    pl.when(high)(open_high)
+    pl.when(part == 3)(open_last)
+    pl.when(inner_high)(open_high)
     for peer in range(n):
         build(0, peer)
         if peer < half:
             pl.when(high)(lambda peer=peer: give(tok, got, 0, 0, 1, peer))
+    pl.when(inner_low)(open_low)
     for row in range(1, rows):
         cell_loads[row].wait()
         for peer in range(n):
             build(row, peer)
-
-    def near(step, carry):
-        give(tok, got, 0, 0, 0, mine + lax.rem(me - mine + step, half))
-        return carry
-
-    def open_low():
-        pl.semaphore_wait(barrier, n - 1)
-
-    def tell(ahead):
-        pl.semaphore_signal(
-            all_sem, inc=1, device_id={"feat": me + ahead}, device_id_type=MESH
-        )
-
-    def tell_high():
-        tell(quarter)
-        tell(half)
+    pl.when(part == 0)(open_outer)
+    pl.when(inner_low | inner_high)(wait_all)
 
     def first_low():
         spread(tok, got, 0, 0)
 
-    def first_high():
-        pl.semaphore_wait(all_sem, 1)
+    def first_rest():
         lax.fori_loop(1, half, near, 0)
 
-    low = jnp.logical_not(high)
-    pl.when(low)(open_low)
-    pl.when(low & (me >= half - quarter))(tell_high)
-    pl.when(low)(first_low)
-    pl.when(high)(first_high)
+    def first_beyond():
+        lax.fori_loop(0, quarter, beyond, 0)
+
+    pl.when(part == 0)(first_low)
+    pl.when(part > 0)(first_rest)
+    pl.when(inner_low)(first_beyond)
     for row in range(1, rows):
         spread(tok, got, 0, row)
     for row in range(rows):
@@ -270,27 +297,30 @@
         context = turned[...].T
         ctx[row] = pack(context.reshape(n, feats, width), packed).astype(BF16)
         spread(ctx, back, 1, row)
-        back[row, pl.ds(me, 1)] = ctx[row, pl.ds(me, 1)]
+        pltpu.make_async_copy(
+            ctx.at[row, me], back.at[row, me], recv_sems.at[1, row, 0]
+        ).start()
         return carry
 
     lax.fori_loop(0, rows, attention, 0)
 
-    def finish(row, first, count):
-        here = pl.ds(first, count)
+    before = max(rows - 1, 1)
+
+    def finish(step, carry):
+        row = jnp.where(inner_high, step // 2, step % rows)
+        side = jnp.where(inner_high, 1 - step % 2, step // rows)
+        row = jnp.where(part == 0, jnp.where(step < 2 * before, step % before, rows - 1), row)
+        side = jnp.where(part == 0, step // before % 2, side)
+        settle(back, recv_sems.at[1, row, side], row, half)
+        here = pl.ds(jnp.where(side == 0, mine, other), half)
         done[row, here] = feed(
             back[row, here], tok[row, here], w_out, gain_two, w_up, w_down, feats, width, packed
-        ).reshape(count, feats, width)
-
-    def whole(row, carry):
-        arrive(back, 1, row, 0)
-        arrive(back, 1, row, 1)
-        finish(row, 0, n)
+        ).reshape(half, feats, width)
         return carry
 
-    lax.fori_loop(0, rows - 1, whole, 0)
-    arrive(back, 1, rows - 1, 0)
-    finish(rows - 1, mine, half)
-    arrive(back, 1, rows - 1, 1)
+    lax.fori_loop(0, 2 * rows - 1, finish, 0)
+    settle(back, recv_sems.at[1, rows - 1, jnp.where(inner_high, 0, 1)], rows - 1, half)
+
     for row in range(rows):
         settle(tok, send_sems.at[0, row], row, n - 1)
         settle(ctx, send_sems.at[1, row], row, n - 1)

time: 32.8 us -> 32.3 us (0.985)
  Pallas kernels: 32.6 us -> 32.1 us
    pallas_call x1, Pallas kernels: 31 us -> 30.5 us  [body(): pl.pallas_call(functools.partial(kernel, n, rows, feats, width, packed),...]
where the time goes in v3:
time: 32.3 us; the launch traced here: 32.1 us
  Pallas kernels  32.1 us (99%)
    pallas_call x1, Pallas kernels, body(): pl.pallas_call(functools.partial(kernel, n, rows, feats, width, packed),...  30.5 us
    pallas_call x1, Pallas kernels, body(): pl.pallas_call(functools.partial(close, n, rows, feats, width, packed), o...  1.6 us

profile of v3, /device:TPU:0, one launch (start us, length us, event | category | flops | bytes accessed | tf_op | source)
XLA Modules:
  0.0 32.1 jit_solution(7804595007624253482)
XLA Ops:
  0.0 30.5 %shard_map.109 = (f32[3,16,32,192]{3,2,1,0:T(8,128)S(1)}, bf16[3,16,48,128]{3,2,1,0:T(8,128)(2,1)S(1)}, bf16[3,16,48,128]{3,2,1,0:T(8,128)(2,1)S(1)}, bf16[192,1...) custom-call(bf16[16,3,32,192]{3,2,1,0:T(8,128)(2,1)} %bitcast.8, ...), custom_call_target="tpu_custom_call" | custom-call | tf_op jit(solution)/shard_map/pallas_call | solution.py:352
  30.5 1.6 %shard_map.110 = f32[16,3,32,192]{3,2,1,0:T(8,128)} custom-call(f32[3,16,32,192]{3,2,1,0:T(8,128)S(1)} %get-tuple-element.12.refs_0_, bf16[3,16,48,128]{3,2,1,0:T(8,128)(2,1)S(1)} %get-tuple-element.13.refs_1_, bf16[3,16,48,128]{3,2,1,0:T(8,128)(2,1)S(1)} %get-tuple-element.14.refs_2_, bf16[192,192]{1,0:T(8,128)(2,1)S(1)} %get-tuple-element.15.refs_3_, ...), custom_call_target="tpu_custom_call" | custom-call | tf_op jit(solution)/shard_map/pallas_call | solution.py:379

commit v4 on v3

--- a/solution.py
+++ b/solution.py
@@ -90,20 +90,17 @@
 def close(n, rows, feats, width, packed, *refs):
     done, back, tok, w_out, gain_two, w_up, w_down, out, last, sems = refs
     half = n // 2
-    quarter = half // 2
-    me = lax.axis_index("feat")
-    mine = me // half * half
+    mine = lax.axis_index("feat") // half * half
     other = half - mine
-    inner_high = me // quarter == 2
     final = rows - 1
     copies = [
         pltpu.make_async_copy(done.at[row], out.at[:, row], sems.at[row]) for row in range(final)
     ]
-    here = pl.ds(jnp.where(inner_high, other, mine), half)
+    here = pl.ds(mine, half)
     copies.append(pltpu.make_async_copy(done.at[final, here], out.at[here, final], sems.at[final]))
     for copy in copies:
         copy.start()
-    here = pl.ds(jnp.where(inner_high, mine, other), half)
+    here = pl.ds(other, half)
     last[...] = feed(
         back[final, here], tok[final, here], w_out, gain_two, w_up, w_down, feats, width, packed
     ).reshape(half, feats, width)
@@ -117,7 +114,8 @@
     sources, refs = refs[:11], refs[11:]
     done, back, tok, w_out, gain_two, w_up, w_down = refs[:7]
     held, refs = refs[7:14] + (w_out, gain_two, w_up, w_down), refs[14:]
-    got, ctx, wqv_t, keys, query, value, turned, even, odd, load_sems, cell_sems, send_sems, recv_sems, all_sem = refs
+    got, ctx, wqv_t, keys, query, value, turned, even, odd = refs[:9]
+    load_sems, cell_sems, send_sems, recv_sems, all_sem = refs[9:]
     (cells, missing, feat_ids, feat_table, nan_embed) = held[:5]
     gain_one, w_qkv = held[5:7]
     scores = (even, odd)
@@ -161,10 +159,15 @@
         load.wait()
 
     ncat = feat_table.shape[0]
-    hot = (lax.broadcasted_iota(jnp.int32, (ncat, feats), 0) == feat_ids[...]).astype(F32)
+    hot = (lax.broadcasted_iota(jnp.int32, (ncat, feats), 0) == feat_ids[...]).astype(BF16)
+    table = feat_table[...]
+    parts = []
+    for _ in range(3):
+        parts.append(table.astype(BF16))
+        table = table - parts[-1].astype(F32)
     femb = lax.dot_general(
-        hot, feat_table[...], (((0,), (0,)), ((), ())),
-        precision=lax.Precision.HIGHEST, preferred_element_type=F32,
+        jnp.concatenate([hot] * 3, axis=0), jnp.concatenate(parts, axis=0),
+        (((0,), (0,)), ((), ())), preferred_element_type=F32,
     )
     nan = nan_embed[...]
     absent = missing[...].astype(F32)
@@ -179,7 +182,7 @@
             device_id_type=MESH,
         ).start()
 
-    def spread(source, target, kind, row):
+    def spread(source, target, kind, row, spans=((1, n),)):
         def one(step, carry):
             peer = me + step
             peer = jnp.where(peer < n, peer, peer - n)
@@ -187,7 +190,8 @@
             give(source, target, kind, row, side, peer)
             return carry
 
-        lax.fori_loop(1, n, one, 0)
+        for start, stop in spans:
+            lax.fori_loop(start, stop, one, 0)
 
     def settle(ref, sem, row, count):
         piece = ref.at[row, pl.ds(0, count)]
@@ -255,8 +259,16 @@
     pl.when(part == 0)(open_outer)
     pl.when(inner_low | inner_high)(wait_all)
 
+    lane = me - part * quarter
+    far_first = (
+        (1, 2 * quarter - lane),
+        (3 * quarter - lane, n - lane),
+        (2 * quarter - lane, 3 * quarter - lane),
+        (n - lane, n),
+    )
+
     def first_low():
-        spread(tok, got, 0, 0)
+        spread(tok, got, 0, 0, far_first)
 
     def first_rest():
         lax.fori_loop(1, half, near, 0)
@@ -268,7 +280,8 @@
     pl.when(part > 0)(first_rest)
     pl.when(inner_low)(first_beyond)
     for row in range(1, rows):
-        spread(tok, got, 0, row)
+        pl.when(part == 0)(lambda row=row: spread(tok, got, 0, row, far_first))
+        pl.when(part > 0)(lambda row=row: spread(tok, got, 0, row))
     for row in range(rows):
         got[row, pl.ds(me, 1)] = tok[row, pl.ds(me, 1)]
     for load in loads[4:]:
@@ -281,6 +294,18 @@
     count = n * feats
     query[...] = jnp.zeros_like(query)
     value[...] = jnp.ones_like(value)
+
+    wide = head_dim * (128 // head_dim)
+
+    def place(row, values, column):
+        values = values.reshape(n, feats, values.shape[-1]).astype(F32)
+        if not packed:
+            ctx[row, :, :, column : column + values.shape[-1]] = values.astype(BF16)
+        elif column == 0:
+            ctx[row, :, 0:feats] = values.astype(BF16)
+        else:
+            values = jnp.concatenate([values[:, : feats // 2], values[:, feats // 2 :]], axis=-1)
+            ctx[row, :, feats : feats + feats // 2] = values.astype(BF16)
 
     def attention(row, carry):
         arrive(got, 0, row, 0)
@@ -294,8 +319,9 @@
             turned[head * head_dim : (head + 1) * head_dim] = weigh(
                 scores[head % 2][...], value, head, head_dim
             )
-        context = turned[...].T
-        ctx[row] = pack(context.reshape(n, feats, width), packed).astype(BF16)
+            if (head + 1) * head_dim == wide:
+                place(row, turned[:wide].T, 0)
+        place(row, turned[wide:].T, wide)
         spread(ctx, back, 1, row)
         pltpu.make_async_copy(
             ctx.at[row, me], back.at[row, me], recv_sems.at[1, row, 0]
@@ -308,7 +334,7 @@
 
     def finish(step, carry):
         row = jnp.where(inner_high, step // 2, step % rows)
-        side = jnp.where(inner_high, 1 - step % 2, step // rows)
+        side = jnp.where(inner_high, step % 2, step // rows)
         row = jnp.where(part == 0, jnp.where(step < 2 * before, step % before, rows - 1), row)
         side = jnp.where(part == 0, step // before % 2, side)
         settle(back, recv_sems.at[1, row, side], row, half)
@@ -319,7 +345,7 @@
         return carry
 
     lax.fori_loop(0, 2 * rows - 1, finish, 0)
-    settle(back, recv_sems.at[1, rows - 1, jnp.where(inner_high, 0, 1)], rows - 1, half)
+    settle(back, recv_sems.at[1, rows - 1, 1], rows - 1, half)
 
     for row in range(rows):
         settle(tok, send_sems.at[0, row], row, n - 1)

time: 32.3 us -> 32.3 us (level)
  no operation moved by 1% of the time
where the time goes in v4:
time: 32.3 us; the launch traced here: 32.1 us
  Pallas kernels  32.1 us (99%)
    pallas_call x1, Pallas kernels, body(): pl.pallas_call(functools.partial(kernel, n, rows, feats, width, packed),...  30.5 us
    pallas_call x1, Pallas kernels, body(): pl.pallas_call(functools.partial(close, n, rows, feats, width, packed), o...  1.6 us

profile of v4, /device:TPU:0, one launch (start us, length us, event | category | flops | bytes accessed | tf_op | source)
XLA Modules:
  0.0 32.1 jit_solution(4203855489632232179)
XLA Ops:
  0.0 30.5 %shard_map.109 = (f32[3,16,32,192]{3,2,1,0:T(8,128)S(1)}, bf16[3,16,48,128]{3,2,1,0:T(8,128)(2,1)S(1)}, bf16[3,16,48,128]{3,2,1,0:T(8,128)(2,1)S(1)}, bf16[192,1...) custom-call(bf16[16,3,32,192]{3,2,1,0:T(8,128)(2,1)} %bitcast.8, ...), custom_call_target="tpu_custom_call" | custom-call | tf_op jit(solution)/shard_map/pallas_call | solution.py:378
  30.5 1.6 %shard_map.110 = f32[16,3,32,192]{3,2,1,0:T(8,128)} custom-call(f32[3,16,32,192]{3,2,1,0:T(8,128)S(1)} %get-tuple-element.12.refs_0_, bf16[3,16,48,128]{3,2,1,0:T(8,128)(2,1)S(1)} %get-tuple-element.13.refs_1_, bf16[3,16,48,128]{3,2,1,0:T(8,128)(2,1)S(1)} %get-tuple-element.14.refs_2_, bf16[192,192]{1,0:T(8,128)(2,1)S(1)} %get-tuple-element.15.refs_3_, ...), custom_call_target="tpu_custom_call" | custom-call | tf_op jit(solution)/shard_map/pallas_call | solution.py:405
